TPU v7x, 32 devices: a whole 2x2x4 slice. The times are simulated.
32 devices in a mesh: row: 4 (over y, x), col: 8 (over z, core).
Axes of the slice: x: 2, y: 2, z: 4, core: 2. Of those that a mesh axis runs over, the one named last changes fastest.
Arguments:
- iterates: float32 [11, 1024], P(None, ('col', 'row')), may hold values from -6 to 6
- residuals: float32 [11, 1024], P(None, ('col', 'row')), may hold values from -3 to 3
- operator: float32 [16384, 1024], P('row', 'col'), may hold values from -0.1875 to 0.1875
- target: float32 [16384], replicated, may hold values from -6 to 6
- cone_id: int32 [16384], replicated, may hold values from 0 to 2047, never falling along the last dimension, each value on 1 to 16 neighbouring positions
Outputs:
- next_point: float32 [1024], P(('col', 'row'))
- projected: float32 [16384], P('row')
Inputs may be any that keep to these rules, and one draw needn't show every extreme that they name: cone_id never falls along the rows; each of the 2048 cones holds 1 to 16 consecutive rows.
All inputs are finite; a program needn't handle non-finite values.
Results may differ from a plain program's by a relative error of at most 0.0003.
Values sent between devices are 32-bit elements; how exact they have to be, the bound alone decides.
No kernel may reach another device: no remote copies, remote signals or barrier semaphores. Data moves between devices by JAX's collectives and lax.ppermute only.
A program may use at most 64 MiB of HBM per device.

v0:
```python
import math
import jax
import jax.numpy as jnp
from jax import lax
from jax.sharding import PartitionSpec as P

HIGH = lax.Precision.HIGHEST
RIM = 16


def with_halo(x, sides, width):
    for axis, dim in sides:
        devices, length = (lax.axis_size(axis), x.shape[dim])
        up = [(i, (i + 1) % devices) for i in range(devices - 1)]
        down = [(j, i) for i, j in up]
        last = lax.slice_in_dim(x, length - width, length, axis=dim)
        leading = lax.slice_in_dim(x, 0, width, axis=dim)
        before = lax.ppermute(last, axis, up)
        after = lax.ppermute(leading, axis, down)
        x = jnp.concatenate([before, x, after], axis=dim)
    return x


def solve_weights(gram, right_side):
    count = gram.shape[0]
    shifted = gram + 0.01 * (jnp.trace(gram) / count) * jnp.eye(count, dtype=jnp.float32)
    factor = jnp.linalg.cholesky(shifted)
    return jax.scipy.linalg.cho_solve((factor, True), right_side)


def window_cones(slack_ext, ids_ext, head_ext, length):
    shifts = range(1 - RIM, RIM)
    slack_win = jnp.stack([slack_ext[RIM + s : RIM + s + length] for s in shifts])
    ids_win = jnp.stack([ids_ext[RIM + s : RIM + s + length] for s in shifts])
    head_win = jnp.stack([head_ext[RIM + s : RIM + s + length] for s in shifts])
    own_ids = ids_ext[RIM : RIM + length]
    slack = slack_ext[RIM : RIM + length]
    head_own = head_ext[RIM : RIM + length]
    same = (ids_win == own_ids[None, :]).astype(jnp.float32)
    head_row = jnp.sum(same * head_win * slack_win, axis=0)
    tail_tot = jnp.sum(same * (1.0 - head_win) * slack_win * slack_win, axis=0)
    norm_row = jnp.sqrt(tail_tot)
    inside = norm_row <= head_row
    killed = norm_row <= -head_row
    safe_norm = jnp.where(norm_row > 0, norm_row, 1.0)
    middle = 0.5 * (head_row + norm_row)
    outside = jnp.where(head_own > 0, middle, middle * slack / safe_norm)
    return jnp.where(inside, slack, jnp.where(killed, 0.0, outside))


def body(iterates, residuals, operator, target, cone_id):
    row_count = lax.axis_size("row")
    col_count = lax.axis_size("col")
    row_block = operator.shape[0]
    local_len = iterates.shape[1]
    all_rows = row_block * row_count
    scale_back = math.sqrt(local_len * row_count * col_count / all_rows)
    row_index = lax.axis_index("row")
    row_offset = row_index * row_block
    delta_x = iterates[1:] - iterates[:-1]
    delta_f = residuals[1:] - residuals[:-1]
    last_f = residuals[-1]
    gram_local = jnp.dot(delta_f, delta_f.T, precision=HIGH)
    side_local = jnp.dot(delta_f, last_f, precision=HIGH)
    anchor = iterates[-1] + last_f
    step_dirs = delta_x + delta_f
    gram, right_side = lax.psum((gram_local, side_local), ("row", "col"))
    weights = solve_weights(gram, right_side)
    blended = anchor - jnp.dot(weights, step_dirs, precision=HIGH)
    columns = operator
    partial_value = jnp.zeros((row_block,), jnp.float32) + jnp.dot(
        columns, lax.all_gather(blended, "row", axis=0, tiled=True), precision=HIGH
    )
    image_own = lax.psum(partial_value, "col")
    head_all = jnp.concatenate(
        [jnp.ones((1,), jnp.float32), (cone_id[1:] != cone_id[:-1]).astype(jnp.float32)]
    )
    ids_pad = jnp.concatenate(
        [jnp.full((RIM,), -1, jnp.int32), cone_id, jnp.full((RIM,), -1, jnp.int32)]
    )
    head_pad = jnp.concatenate(
        [jnp.zeros((RIM,), jnp.float32), head_all, jnp.zeros((RIM,), jnp.float32)]
    )
    ids_ext = lax.dynamic_slice_in_dim(ids_pad, row_offset, row_block + 2 * RIM, 0)
    head_ext = lax.dynamic_slice_in_dim(head_pad, row_offset, row_block + 2 * RIM, 0)
    slack_own = lax.dynamic_slice_in_dim(target, row_offset, row_block, 0) - image_own
    slack_ext = with_halo(slack_own, (("row", 0),), RIM)
    slack_own = slack_ext[RIM : RIM + row_block]
    proj_own = window_cones(slack_ext, ids_ext, head_ext, row_block)
    correction = proj_own - slack_own
    columns = operator
    back = lax.psum_scatter(
        jnp.dot(correction, columns, precision=HIGH), "row", scatter_dimension=0, tiled=True
    )
    next_point = blended - scale_back * back
    return (next_point, proj_own)


def solution(mesh):
    return jax.shard_map(
        body,
        mesh=mesh,
        in_specs=(P(None, ("col", "row")), P(None, ("col", "row")), P("row", "col"), P(), P()),
        out_specs=(P(("col", "row")), P("row")),
        check_vma=False,
    )
```

profile of v0, /device:TPU:0, one launch (start us, length us, event | category | flops | bytes accessed | tf_op | source)
XLA Modules:
  0.0 124.1 jit_solution(8513609570144858646)
XLA Ops:
  0.7 1.0 convolution_bitcast_fusion.3
  1.7 1.0 fusion.48
  2.7 42.1 %all-reduce.2 = (f32[10,10]{0,1:T(8,128)S(1)}, f32[10]{0:T(128)S(1)}) all-reduce(f32[10,10]{0,1:T(8,128)S(1)} %fusion.48, f32[10]{0:T(128)S(1)} %convolution_bitcast_fusion.3), channel_id=1, replica_groups=mesh['row'=4,'col'=8] {'row','col'}, use_global_device_ids=true, to_apply=%region_0.0 | all-reduce | flops 110 | bytes 880 | tf_op jit(solution)/shard_map/psum | solution.py:67
  46.1 0.9 cholesky.17
  48.6 0.8 custom-call.10
  49.7 1.4 %fusion.56 = (u32[1]{0:T(128)}, u32[1]{0:T(128)}) fusion(u32[32]{0:T(128)} %constant.89, u32[]{:T(128)S(6)} %add.52, u32[]{:T(128)S(6)} %add.49), kind=kLoop, calls=%fused_computation.136 | loop fusion | bytes 24
  51.7 0.9 fusion
  53.1 9.7 %all-reduce = f32[128]{0:T(128)S(1)} all-reduce(f32[128]{0:T(128)S(1)} %dynamic-update-slice.3), channel_id=1, replica_groups=mesh['row'=4,'col'=8] {'row'}, use_global_device_ids=true, to_apply=%add | all-reduce | flops 128 | bytes 1024
  62.9 1.8 %fusion.43 = f32[1,4096]{1,0:T(1,128)S(1)} fusion(f32[4096,128]{1,0:T(8,128)S(1)} %copy-done, f32[128]{0:T(128)S(1)} %all-reduce), kind=kOutput, calls=%fused_computation.123 | convolution fusion | flops 6291456 | bytes 2114048 | tf_op jit(solution)/shard_map/dot_general | solution.py:71
  64.7 25.9 %psum.23 = f32[4096]{0:T(1024)S(1)} all-reduce(f32[4096]{0:T(1024)S(1)} %bitcast.210), channel_id=1, replica_groups=mesh['row'=4,'col'=8] {'col'}, use_global_device_ids=true, to_apply=%region_5.6 | all-reduce | flops 4096 | bytes 32768 | tf_op jit(solution)/shard_map/psum | solution.py:74
  90.6 0.7 dynamic-slice_subtract_fusion
  91.9 1.3 %collective-permute-start.1 = (f32[16]{0:T(128)}, f32[16]{0:T(128)}, u32[]{:S(2)}, u32[]{:S(2)}) collective-permute-start(f32[16]{0:T(128)} %get-tuple-element.100), channel_id=1, source_target_pairs={{8,0},{16,8},{24,16},{9,1},{17,9},{25,17},{10,2},{18,10},{26,18},{... | collective-permute-start | bytes 200 | tf_op jit(solution)/shard_map/ppermute | solution.py:19
  93.2 5.1 %collective-permute-start = (f32[16]{0:T(128)}, f32[16]{0:T(128)}, u32[]{:S(2)}, u32[]{:S(2)}) collective-permute-start(f32[16]{0:T(128)} %get-tuple-element.101), channel_id=1, source_target_pairs={{0,8},{8,16},{16,24},{1,9},{9,17},{17,25},{2,10},{10,18},{18,26},{... | collective-permute-start | bytes 200 | tf_op jit(solution)/shard_map/ppermute | solution.py:18
  98.6 0.8 fusion.54
  100.8 0.8 stack.351
  101.5 1.6 %stack.319 = s32[31,4096]{1,0:T(8,128)S(1)} concatenate(s32[1,4096]{1,0:T(1,128)} %bitcast.224, s32[1,4096]{1,0:T(1,128)} %bitcast.223, s32[1,4096]{1,0:T(1,128)} %bitcast.222, s32[1,4096]{1,0:T(1,128)} %bitcast.221, s32[1,4096]{1,0:T(1,128)} %bitcast.220, s32[1,4096]{1,0:T(1,128)} %bitcast.219, s32[1,4096]{1,0:T(1,128)} %bitcast.218, s32[1,4096]{1,0:T(1,128)} %bitcast.217, ...), dimensions={0} | concatenate | bytes 1015808 | tf_op jit(solution)/shard_map/stack | solution.py:34
  103.1 1.1 pad_maximum_fusion
  104.2 1.0 fusion.3
  105.2 1.0 fusion.17
  106.2 1.7 %pad_maximum_fusion.1 = (f32[4096]{0:T(1024)S(1)}, f32[4096]{0:T(1024)}, f32[4096]{0:T(1024)}, f32[4096]{0:T(1024)}, f32[4096]{0:T(1024)}, /*index=5*/f32[4096]{...) fusion(f32[4096]{0:T(1024)S(1)} %dynamic-slice_subtract_fusion, f32[16]{0:T(128)} %collective-permute-done), kind=kLoop, calls=%fused_computation.102 | loop fusion | flops 36864 | bytes 163904 | tf_op jit(solution)/shard_map/concatenate | solution.py:20
  108.0 4.1 %stack.383 = f32[31,4096]{1,0:T(8,128)} concatenate(f32[1,4096]{1,0:T(1,128)} %bitcast.202, f32[1,4096]{1,0:T(1,128)} %bitcast.203, f32[1,4096]{1,0:T(1,128)} %bitcast.204, f32[1,4096]{1,0:T(1,128)} %bitcast.205, f32[1,4096]{1,0:T(1,128)} %bitcast.206, f32[1,4096]{1,0:T(1,128)} %bitcast.207, f32[1,4096]{1,0:T(1,128)} %bitcast.208, f32[1,4096]{1,0:T(1,128)} %bitcast.209, ...), dimensions={0} | concatenate | bytes 1015808 | tf_op jit(solution)/shard_map/stack | solution.py:33
  112.1 1.3 %fusion.1 = (f32[4096]{0:T(1024)S(1)}, f32[4096]{0:T(1024)S(1)}) fusion(f32[31,4096]{1,0:T(8,128)} %stack.383, f32[31,4096]{1,0:T(8,128)S(1)} %stack.351, s32[31,4096]{1,0:T(8,128)S(1)} %stack.319, s32[4096]{0:T(1024)S(1)} %get-tuple-element.54), kind=kLoop, calls=%fused_computation.7 | loop fusion | flops 1134592 | bytes 1572864 | tf_op jit(solution)/shard_map/reduce_sum | solution.py:41
  114.0 1.1 convolution_bitcast_fusion.4
  115.1 8.4 %all-reduce.1 = f32[128]{0:T(128)S(1)} all-reduce(f32[128]{0:T(128)S(1)} %convolution_bitcast_fusion.4), channel_id=2, replica_groups=mesh['row'=4,'col'=8] {'row'}, use_global_device_ids=true, to_apply=%region_8.9.clone | all-reduce | flops 128 | bytes 1024
  (34 shorter events, 5.9 us)
Async XLA Ops:
  0.6 62.2 %copy-start = (f32[4096,128]{1,0:T(8,128)S(1)}, f32[4096,128]{1,0:T(8,128)}, u32[]{:S(2)}) copy-start(f32[4096,128]{1,0:T(8,128)} %param.7) | copy-start | bytes 6291460
  0.6 97.7 %copy-start.1 = (s32[16384]{0:T(1024)S(1)}, s32[16384]{0:T(1024)}, u32[]{:S(2)}) copy-start(s32[16384]{0:T(1024)} %param.9) | copy-start | bytes 196612
  52.6 0.5 copy-start.2
  91.9 11.2 %collective-permute-start.1 = (f32[16]{0:T(128)}, f32[16]{0:T(128)}, u32[]{:S(2)}, u32[]{:S(2)}) collective-permute-start(f32[16]{0:T(128)} %get-tuple-element.100), channel_id=1, source_target_pairs={{8,0},{16,8},{24,16},{9,1},{17,9},{25,17},{10,2},{18,10},{26,18},{... | collective-permute-start | bytes 200 | tf_op jit(solution)/shard_map/ppermute | solution.py:19
  93.2 12.0 %collective-permute-start = (f32[16]{0:T(128)}, f32[16]{0:T(128)}, u32[]{:S(2)}, u32[]{:S(2)}) collective-permute-start(f32[16]{0:T(128)} %get-tuple-element.101), channel_id=1, source_target_pairs={{0,8},{8,16},{16,24},{1,9},{9,17},{17,25},{2,10},{10,18},{18,26},{... | collective-permute-start | bytes 200 | tf_op jit(solution)/shard_map/ppermute | solution.py:18
  112.1 11.4 %copy-start.3 = (f32[32]{0:T(128)S(1)}, f32[32]{0:T(128)}, u32[]{:S(2)}) copy-start(f32[32]{0:T(128)} %copy-done.2) | copy-start | bytes 388
where the time goes:
time: 125 us; the launch traced here: 124 us
  blocking collectives  86.1 us (69%)
  other arithmetic  11.8 us (9%)
  local copies, waits for them, and re-layouts  10.9 us (9%)
  starting transfers between devices  6.42 us (5%)
  matrix products  6.11 us (5%)
  between operations  2.75 us (2%)
    psum x1, blocking collectives, body(): gram, right_side = lax.psum((gram_local, side_local), ('row', 'col'))  42.1 us
    psum x1, blocking collectives, body(): image_own = lax.psum(partial_value, 'col')  25.9 us
    unnamed x2, blocking collectives  18.1 us
    ppermute x1, starting transfers between devices, with_halo(): before = lax.ppermute(last, axis, up)  5.14 us
    concatenate x4, other arithmetic, with_halo(): x = jnp.concatenate([before, x, after], axis=dim)  4.81 us
    another operation x1, local copies, waits for them, and re-layouts, window_cones(): slack_win = jnp.stack([slack_ext[RIM + s:RIM + s + length] for s in shifts])  4.14 us
  transfers between devices with their start and end apart: 2, of which 0 were waited for; matrix products, arithmetic and copies ran while one was open for 5% of the time, Pallas kernels for 0%

commit v1 on v0

--- a/solution.py
+++ b/solution.py
@@ -71,7 +71,7 @@
     partial_value = jnp.zeros((row_block,), jnp.float32) + jnp.dot(
         columns, lax.all_gather(blended, "row", axis=0, tiled=True), precision=HIGH
     )
-    image_own = lax.psum(partial_value, "col")
+    image_own = jnp.sum(lax.all_gather(partial_value, "col"), axis=0)
     head_all = jnp.concatenate(
         [jnp.ones((1,), jnp.float32), (cone_id[1:] != cone_id[:-1]).astype(jnp.float32)]
     )

time: 125 us -> 113 us (0.904)
  blocking collectives: 86.1 us -> 74.1 us
    psum x1 -> x0, blocking collectives: 25.9 us -> none  [body(): image_own = lax.psum(partial_value, 'col')]
    all_gather x0 -> x1, blocking collectives: none -> 14 us  [body(): image_own = jnp.sum(lax.all_gather(partial_value, 'col'), axis=0)]
where the time goes in v1:
time: 113 us; the launch traced here: 112 us
  blocking collectives  74.1 us (66%)
  other arithmetic  11.8 us (10%)
  local copies, waits for them, and re-layouts  11.1 us (10%)
  starting transfers between devices  6.42 us (6%)
  matrix products  6.11 us (5%)
  between operations  2.76 us (2%)
    psum x1, blocking collectives, body(): gram, right_side = lax.psum((gram_local, side_local), ('row', 'col'))  42.1 us
    unnamed x2, blocking collectives  18.1 us
    all_gather x1, blocking collectives, body(): image_own = jnp.sum(lax.all_gather(partial_value, 'col'), axis=0)  14 us
    ppermute x1, starting transfers between devices, with_halo(): before = lax.ppermute(last, axis, up)  5.14 us
    concatenate x4, other arithmetic, with_halo(): x = jnp.concatenate([before, x, after], axis=dim)  4.81 us
    another operation x1, local copies, waits for them, and re-layouts, window_cones(): slack_win = jnp.stack([slack_ext[RIM + s:RIM + s + length] for s in shifts])  4.14 us
  transfers between devices with their start and end apart: 2, of which 0 were waited for; matrix products, arithmetic and copies ran while one was open for 5% of the time, Pallas kernels for 0%

profile of v1, /device:TPU:0, one launch (start us, length us, event | category | flops | bytes accessed | tf_op | source)
XLA Modules:
  0.0 112.4 jit_solution(1452194952120421009)
XLA Ops:
  0.7 1.0 convolution_bitcast_fusion.3
  1.7 1.0 fusion.48
  2.7 42.1 %all-reduce.2 = (f32[10,10]{0,1:T(8,128)S(1)}, f32[10]{0:T(128)S(1)}) all-reduce(f32[10,10]{0,1:T(8,128)S(1)} %fusion.48, f32[10]{0:T(128)S(1)} %convolution_bitcast_fusion.3), channel_id=1, replica_groups=mesh['row'=4,'col'=8] {'row','col'}, use_global_device_ids=true, to_apply=%region_0.0 | all-reduce | flops 110 | bytes 880 | tf_op jit(solution)/shard_map/psum | solution.py:67
  46.1 0.9 cholesky.17
  48.6 0.8 custom-call.10
  49.7 1.4 %fusion.56 = (u32[1]{0:T(128)}, u32[1]{0:T(128)}) fusion(u32[32]{0:T(128)} %constant.89, u32[]{:T(128)S(6)} %add.50, u32[]{:T(128)S(6)} %add.47), kind=kLoop, calls=%fused_computation.136 | loop fusion | bytes 24
  51.7 0.9 fusion
  53.3 9.7 %all-reduce = f32[128]{0:T(128)S(1)} all-reduce(f32[128]{0:T(128)S(1)} %dynamic-update-slice.3), channel_id=1, replica_groups=mesh['row'=4,'col'=8] {'row'}, use_global_device_ids=true, to_apply=%add | all-reduce | flops 128 | bytes 1024
  63.0 1.8 %fusion.43 = f32[1,4096]{1,0:T(1,128)S(1)} fusion(f32[4096,128]{1,0:T(8,128)S(1)} %copy-done, f32[128]{0:T(128)S(1)} %all-reduce), kind=kOutput, calls=%fused_computation.123 | convolution fusion | flops 6291456 | bytes 2114048 | tf_op jit(solution)/shard_map/dot_general | solution.py:71
  64.8 14.0 %all-gather = f32[32768]{0:T(1024)S(1)} all-gather(f32[4096]{0:T(1024)S(1)} %bitcast.210), channel_id=2, replica_groups=mesh['row'=4,'col'=8] {'col'}, dimensions={0}, use_global_device_ids=true | all-gather | bytes 147456 | tf_op jit(solution)/shard_map/all_gather | solution.py:74
  78.9 0.7 dynamic-slice_subtract_fusion
  80.2 1.3 %collective-permute-start.1 = (f32[16]{0:T(128)}, f32[16]{0:T(128)}, u32[]{:S(2)}, u32[]{:S(2)}) collective-permute-start(f32[16]{0:T(128)} %get-tuple-element.100), channel_id=1, source_target_pairs={{8,0},{16,8},{24,16},{9,1},{17,9},{25,17},{10,2},{18,10},{26,18},{... | collective-permute-start | bytes 200 | tf_op jit(solution)/shard_map/ppermute | solution.py:19
  81.5 5.1 %collective-permute-start = (f32[16]{0:T(128)}, f32[16]{0:T(128)}, u32[]{:S(2)}, u32[]{:S(2)}) collective-permute-start(f32[16]{0:T(128)} %get-tuple-element.101), channel_id=1, source_target_pairs={{0,8},{8,16},{16,24},{1,9},{9,17},{17,25},{2,10},{10,18},{18,26},{... | collective-permute-start | bytes 200 | tf_op jit(solution)/shard_map/ppermute | solution.py:18
  86.9 0.8 fusion.54
  89.1 0.8 stack.351
  89.8 1.6 %stack.319 = s32[31,4096]{1,0:T(8,128)S(1)} concatenate(s32[1,4096]{1,0:T(1,128)} %bitcast.224, s32[1,4096]{1,0:T(1,128)} %bitcast.223, s32[1,4096]{1,0:T(1,128)} %bitcast.222, s32[1,4096]{1,0:T(1,128)} %bitcast.221, s32[1,4096]{1,0:T(1,128)} %bitcast.220, s32[1,4096]{1,0:T(1,128)} %bitcast.219, s32[1,4096]{1,0:T(1,128)} %bitcast.218, s32[1,4096]{1,0:T(1,128)} %bitcast.217, ...), dimensions={0} | concatenate | bytes 1015808 | tf_op jit(solution)/shard_map/stack | solution.py:34
  91.4 1.1 pad_maximum_fusion
  92.5 1.0 fusion.3
  93.5 1.0 fusion.17
  94.5 1.7 %pad_maximum_fusion.1 = (f32[4096]{0:T(1024)S(1)}, f32[4096]{0:T(1024)}, f32[4096]{0:T(1024)}, f32[4096]{0:T(1024)}, f32[4096]{0:T(1024)}, /*index=5*/f32[4096]{...) fusion(f32[4096]{0:T(1024)S(1)} %dynamic-slice_subtract_fusion, f32[16]{0:T(128)} %collective-permute-done), kind=kLoop, calls=%fused_computation.102 | loop fusion | flops 36864 | bytes 163904 | tf_op jit(solution)/shard_map/concatenate | solution.py:20
  96.3 4.1 %stack.383 = f32[31,4096]{1,0:T(8,128)} concatenate(f32[1,4096]{1,0:T(1,128)} %bitcast.202, f32[1,4096]{1,0:T(1,128)} %bitcast.203, f32[1,4096]{1,0:T(1,128)} %bitcast.204, f32[1,4096]{1,0:T(1,128)} %bitcast.205, f32[1,4096]{1,0:T(1,128)} %bitcast.206, f32[1,4096]{1,0:T(1,128)} %bitcast.207, f32[1,4096]{1,0:T(1,128)} %bitcast.208, f32[1,4096]{1,0:T(1,128)} %bitcast.209, ...), dimensions={0} | concatenate | bytes 1015808 | tf_op jit(solution)/shard_map/stack | solution.py:33
  100.4 1.3 %fusion.1 = (f32[4096]{0:T(1024)S(1)}, f32[4096]{0:T(1024)S(1)}) fusion(f32[31,4096]{1,0:T(8,128)} %stack.383, f32[31,4096]{1,0:T(8,128)S(1)} %stack.351, s32[31,4096]{1,0:T(8,128)S(1)} %stack.319, s32[4096]{0:T(1024)S(1)} %get-tuple-element.54), kind=kLoop, calls=%fused_computation.7 | loop fusion | flops 1134592 | bytes 1572864 | tf_op jit(solution)/shard_map/reduce_sum | solution.py:41
  102.3 1.1 convolution_bitcast_fusion.4
  103.4 8.4 %all-reduce.1 = f32[128]{0:T(128)S(1)} all-reduce(f32[128]{0:T(128)S(1)} %convolution_bitcast_fusion.4), channel_id=3, replica_groups=mesh['row'=4,'col'=8] {'row'}, use_global_device_ids=true, to_apply=%region_8.9.clone | all-reduce | flops 128 | bytes 1024
  (36 shorter events, 6.2 us)
Async XLA Ops:
  0.6 62.4 %copy-start = (f32[4096,128]{1,0:T(8,128)S(1)}, f32[4096,128]{1,0:T(8,128)}, u32[]{:S(2)}) copy-start(f32[4096,128]{1,0:T(8,128)} %param.7) | copy-start | bytes 6291460
  0.6 86.0 %copy-start.1 = (s32[16384]{0:T(1024)S(1)}, s32[16384]{0:T(1024)}, u32[]{:S(2)}) copy-start(s32[16384]{0:T(1024)} %param.9) | copy-start | bytes 196612
  52.6 0.5 copy-start.2
  80.2 11.2 %collective-permute-start.1 = (f32[16]{0:T(128)}, f32[16]{0:T(128)}, u32[]{:S(2)}, u32[]{:S(2)}) collective-permute-start(f32[16]{0:T(128)} %get-tuple-element.100), channel_id=1, source_target_pairs={{8,0},{16,8},{24,16},{9,1},{17,9},{25,17},{10,2},{18,10},{26,18},{... | collective-permute-start | bytes 200 | tf_op jit(solution)/shard_map/ppermute | solution.py:19
  81.5 12.0 %collective-permute-start = (f32[16]{0:T(128)}, f32[16]{0:T(128)}, u32[]{:S(2)}, u32[]{:S(2)}) collective-permute-start(f32[16]{0:T(128)} %get-tuple-element.101), channel_id=1, source_target_pairs={{0,8},{8,16},{16,24},{1,9},{9,17},{17,25},{2,10},{10,18},{18,26},{... | collective-permute-start | bytes 200 | tf_op jit(solution)/shard_map/ppermute | solution.py:18
  100.4 11.4 %copy-start.3 = (f32[32]{0:T(128)S(1)}, f32[32]{0:T(128)}, u32[]{:S(2)}) copy-start(f32[32]{0:T(128)} %copy-done.2) | copy-start | bytes 388
